TPU v7x, 32 devices: a whole 2x2x4 slice. The times are simulated.
32 devices in a mesh: shard: 8 (over z, y), tensor: 2 (over core), context: 2 (over x).
Axes of the slice: x: 2, y: 2, z: 4, core: 2. Of those that a mesh axis runs over, the one named last changes fastest.
Arguments:
- hidden_in: bfloat16 [16, 1024, 1280], P(('shard', 'tensor'), 'context'), may hold values from -6 to 6
- patch_rows: int32 [16, 1024], P('shard', 'context'), may hold values from 0 to 63
- patch_cols: int32 [16, 1024], P('shard', 'context'), may hold values from 0 to 63
- attn_norm_gain: float32 [1280], replicated, may hold values from 0.5 to 1.5
- attn_norm_bias: float32 [1280], replicated, may hold values from -1.2 to 1.2
- query_key_value_weight: bfloat16 [1280, 3, 1280], P(('shard', 'context'), None, 'tensor'), may hold values from -0.15625 to 0.15625
- query_key_value_bias: float32 [3, 1280], replicated, may hold values from -1.2 to 1.2
- out_weight: bfloat16 [1280, 1280], P('tensor', ('shard', 'context')), may hold values from -2.5 to 2.5
- out_bias: float32 [1280], replicated, may hold values from -1.2 to 1.2
- mlp_norm_gain: float32 [1280], replicated, may hold values from 0.5 to 1.5
- mlp_norm_bias: float32 [1280], replicated, may hold values from -1.2 to 1.2
- fc1_weight: bfloat16 [1280, 5120], P(('shard', 'context'), 'tensor'), may hold values from -0.15625 to 0.15625
- fc1_bias: float32 [5120], replicated, may hold values from -1.2 to 1.2
- fc2_weight: bfloat16 [5120, 1280], P('tensor', ('shard', 'context')), may hold values from -0.078125 to 0.078125
- fc2_bias: float32 [1280], replicated, may hold values from -1.2 to 1.2
- cotangent: bfloat16 [16, 1024, 1280], P(('shard', 'tensor'), 'context'), may hold values from -6 to 6
Outputs:
- block_out: bfloat16 [16, 1024, 1280], P(('shard', 'tensor'), 'context')
- grad_input: float32 [16, 1024, 1280], P(('shard', 'tensor'), 'context')
- grad_attn_norm_gain: float32 [1280], replicated
- grad_attn_norm_bias: float32 [1280], replicated
- grad_qkv_weight: float32 [1280, 3, 1280], P(('shard', 'context'), None, 'tensor')
- grad_qkv_bias: float32 [3, 1280], replicated
- grad_out_weight: float32 [1280, 1280], P('tensor', ('shard', 'context'))
- grad_out_bias: float32 [1280], replicated
- grad_mlp_norm_gain: float32 [1280], replicated
- grad_mlp_norm_bias: float32 [1280], replicated
- grad_fc1_weight: float32 [1280, 5120], P(('shard', 'context'), 'tensor')
- grad_fc1_bias: float32 [5120], replicated
- grad_fc2_weight: float32 [5120, 1280], P('tensor', ('shard', 'context'))
- grad_fc2_bias: float32 [1280], replicated
All inputs are finite; a program needn't handle non-finite values.
Results may differ from a plain program's by a relative error of at most 0.015.
Values may be sent and summed in bfloat16 or wider, within the bound.
A program may use at most 192 MiB of HBM per device.

v0:
```python
import jax
import jax.numpy as jnp
from jax import lax
from jax.sharding import PartitionSpec as P

HEAD_DIM = 80


def normalize(field, gain, shift):
    mean_value = jnp.mean(field, axis=-1, keepdims=True)
    centered = field - mean_value
    variance = jnp.mean(centered * centered, axis=-1, keepdims=True)
    inv_scale = lax.rsqrt(variance + 1e-06)
    unit_field = centered * inv_scale
    return (unit_field * gain + shift, unit_field, inv_scale)


def norm_backward(grad_normed, unit_field, inv_scale, gain):
    grad_unit = grad_normed * gain
    mean_grad = jnp.mean(grad_unit, axis=-1, keepdims=True)
    mean_along = jnp.mean(grad_unit * unit_field, axis=-1, keepdims=True)
    grad_field = inv_scale * (grad_unit - mean_grad - unit_field * mean_along)
    return (
        grad_field,
        jnp.sum(grad_normed * unit_field, axis=(0, 1)),
        jnp.sum(grad_normed, axis=(0, 1)),
    )


def rotary_tables(rows_index, cols_index):
    quarter = HEAD_DIM // 4
    frequency = 10000.0 ** (-jnp.arange(quarter, dtype=jnp.float32) / quarter)
    row_angles = rows_index.astype(jnp.float32)[..., None] * frequency
    col_angles = cols_index.astype(jnp.float32)[..., None] * frequency
    angles = jnp.concatenate([row_angles, col_angles, row_angles, col_angles], axis=-1)
    return (jnp.cos(angles)[:, :, None, :], jnp.sin(angles)[:, :, None, :])


def rotate(field, cosine, sine):
    middle_index = field.shape[-1] // 2
    turned = jnp.concatenate([-field[..., middle_index:], field[..., :middle_index]], axis=-1)
    return field * cosine + turned * sine


def rotate_back(grad_field, cosine, sine):
    middle_index = grad_field.shape[-1] // 2
    weighted = grad_field * sine
    turned = jnp.concatenate([weighted[..., middle_index:], -weighted[..., :middle_index]], axis=-1)
    return grad_field * cosine + turned


def attend_forward(inputs):
    queries, keys, values = inputs
    scores = jnp.einsum(
        "phd,khd->hpk", queries, keys, preferred_element_type=jnp.float32
    ) * HEAD_DIM ** (-0.5)
    row_top = jnp.max(scores, axis=-1, keepdims=True)
    expos = jnp.exp(scores - row_top)
    row_total = jnp.sum(expos, axis=-1, keepdims=True)
    weights = (expos / row_total).astype(jnp.bfloat16)
    mixed = jnp.einsum("hpk,khd->phd", weights, values, preferred_element_type=jnp.float32)
    return (mixed, (row_top + jnp.log(row_total))[..., 0])


def attend_backward(inputs):
    queries, keys, values, log_total, grad_mixed = inputs
    scale_factor = HEAD_DIM ** (-0.5)
    scores = (
        jnp.einsum("phd,khd->hpk", queries, keys, preferred_element_type=jnp.float32) * scale_factor
    )
    probs = jnp.exp(scores - log_total[..., None])
    grad_probs = jnp.einsum("phd,khd->hpk", grad_mixed, values, preferred_element_type=jnp.float32)
    inner_sum = jnp.sum(probs * grad_probs, axis=-1, keepdims=True)
    grad_scores = (probs * (grad_probs - inner_sum)).astype(jnp.bfloat16)
    grad_queries = (
        jnp.einsum("hpk,khd->phd", grad_scores, keys, preferred_element_type=jnp.float32)
        * scale_factor
    )
    grad_keys = (
        jnp.einsum("hpk,phd->khd", grad_scores, queries, preferred_element_type=jnp.float32)
        * scale_factor
    )
    grad_values = jnp.einsum(
        "hpk,phd->khd", probs.astype(jnp.bfloat16), grad_mixed, preferred_element_type=jnp.float32
    )
    return (grad_queries, grad_keys, grad_values)


def on_device(
    hidden_in,
    patch_rows,
    patch_cols,
    attn_norm_gain,
    attn_norm_bias,
    query_key_value_weight,
    query_key_value_bias,
    out_weight,
    out_bias,
    mlp_norm_gain,
    mlp_norm_bias,
    fc1_weight,
    fc1_bias,
    fc2_weight,
    fc2_bias,
    cotangent,
):
    local_width = query_key_value_weight.shape[2]
    local_units = fc1_weight.shape[1]
    head_count = local_width // HEAD_DIM
    tensor_rank = lax.axis_index("tensor")
    complete_query_key_value, full_out, full_fc1, full_fc2 = (
        lax.all_gather(query_key_value_weight, ("shard", "context"), axis=0, tiled=True),
        lax.all_gather(out_weight, ("shard", "context"), axis=1, tiled=True),
        lax.all_gather(fc1_weight, ("shard", "context"), axis=0, tiled=True),
        lax.all_gather(fc2_weight, ("shard", "context"), axis=1, tiled=True),
    )
    resid = hidden_in.astype(jnp.float32)
    normed_one, unit_one, scale_one = normalize(resid, attn_norm_gain, attn_norm_bias)
    collected_first_normed = lax.all_gather(
        normed_one.astype(jnp.bfloat16), "tensor", axis=0, tiled=True
    )
    group_images = collected_first_normed.shape[0]
    local_patches = collected_first_normed.shape[1]
    head_shape = (group_images, local_patches, head_count, HEAD_DIM)
    own_qkv_bias = lax.dynamic_slice_in_dim(
        query_key_value_bias, tensor_rank * local_width, local_width, 1
    )
    projection_output = (
        jnp.einsum(
            "bxv,vhl->bxhl",
            collected_first_normed,
            complete_query_key_value,
            preferred_element_type=jnp.float32,
        )
        + own_qkv_bias
    )
    cosine, sine = rotary_tables(patch_rows, patch_cols)
    queries = rotate(projection_output[:, :, 0].reshape(head_shape), cosine, sine).astype(
        jnp.bfloat16
    )
    keys_local = rotate(projection_output[:, :, 1].reshape(head_shape), cosine, sine).astype(
        jnp.bfloat16
    )
    values_local = projection_output[:, :, 2].astype(jnp.bfloat16)
    keys_flat = keys_local.reshape(group_images, local_patches, local_width)
    all_keys, all_values = (
        lax.all_gather(keys_flat, "context", axis=1, tiled=True),
        lax.all_gather(values_local, "context", axis=1, tiled=True),
    )
    image_patches = all_keys.shape[1]
    full_head_shape = (group_images, image_patches, head_count, HEAD_DIM)
    keys_heads = all_keys.reshape(full_head_shape)
    values_heads = all_values.reshape(full_head_shape)
    mixed_heads, log_total = lax.map(attend_forward, (queries, keys_heads, values_heads))
    attn_mixed = mixed_heads.reshape(group_images, local_patches, local_width).astype(jnp.bfloat16)
    shard_portion = attn_mixed
    attn_branch = lax.psum_scatter(
        jnp.einsum(
            "npe,ed->npd", shard_portion, full_out, preferred_element_type=jnp.float32
        ).astype(jnp.bfloat16),
        "tensor",
        scatter_dimension=0,
        tiled=True,
    ).astype(jnp.float32)
    middle = resid + attn_branch + out_bias
    normed_two, unit_two, scale_two = normalize(middle, mlp_norm_gain, mlp_norm_bias)
    gathered_two = lax.all_gather(normed_two.astype(jnp.bfloat16), "tensor", axis=0, tiled=True)
    own_fc1_bias = lax.dynamic_slice_in_dim(fc1_bias, tensor_rank * local_units, local_units, 0)
    pre_act = (
        jnp.einsum("npd,df->npf", gathered_two, full_fc1, preferred_element_type=jnp.float32)
        + own_fc1_bias
    )
    gate_sigmoid = jax.nn.sigmoid(1.702 * pre_act)
    activated = (pre_act * gate_sigmoid).astype(jnp.bfloat16)
    shard_portion = activated
    mlp_branch = lax.psum_scatter(
        jnp.einsum(
            "npf,fd->npd", shard_portion, full_fc2, preferred_element_type=jnp.float32
        ).astype(jnp.bfloat16),
        "tensor",
        scatter_dimension=0,
        tiled=True,
    ).astype(jnp.float32)
    block_out = (middle + mlp_branch + fc2_bias).astype(jnp.bfloat16)
    backward_query_key_value, back_out, back_fc1, back_fc2 = (
        lax.all_gather(query_key_value_weight, ("shard", "context"), axis=0, tiled=True),
        lax.all_gather(out_weight, ("shard", "context"), axis=1, tiled=True),
        lax.all_gather(fc1_weight, ("shard", "context"), axis=0, tiled=True),
        lax.all_gather(fc2_weight, ("shard", "context"), axis=1, tiled=True),
    )
    grad_top = cotangent.astype(jnp.float32)
    fc2_bias_part = jnp.sum(grad_top, axis=(0, 1))
    grad_gathered = lax.all_gather(cotangent, "tensor", axis=0, tiled=True)
    fc2_weight_part = jnp.einsum(
        "npf,npd->fd", activated, grad_gathered, preferred_element_type=jnp.float32
    )
    grad_act = jnp.einsum(
        "npd,fd->npf", grad_gathered, back_fc2, preferred_element_type=jnp.float32
    )
    slope = gate_sigmoid + 1.702 * pre_act * gate_sigmoid * (1.0 - gate_sigmoid)
    grad_pre = (grad_act * slope).astype(jnp.bfloat16)
    fc1_bias_own = jnp.sum(grad_pre, axis=(0, 1), dtype=jnp.float32)
    fc1_weight_part = jnp.einsum(
        "npd,npf->df", gathered_two, grad_pre, preferred_element_type=jnp.float32
    )
    shard_portion = grad_pre
    grad_normed_two = lax.psum_scatter(
        jnp.einsum(
            "npf,df->npd", shard_portion, back_fc1, preferred_element_type=jnp.float32
        ).astype(jnp.bfloat16),
        "tensor",
        scatter_dimension=0,
        tiled=True,
    ).astype(jnp.float32)
    grad_mid_norm, gain_two_part, shift_two_part = norm_backward(
        grad_normed_two, unit_two, scale_two, mlp_norm_gain
    )
    grad_middle = grad_top + grad_mid_norm
    out_bias_part = jnp.sum(grad_middle, axis=(0, 1))
    grad_mid_gathered = lax.all_gather(
        grad_middle.astype(jnp.bfloat16), "tensor", axis=0, tiled=True
    )
    out_weight_part = jnp.einsum(
        "npe,npd->ed", attn_mixed, grad_mid_gathered, preferred_element_type=jnp.float32
    )
    grad_mixed = jnp.einsum(
        "npd,ed->npe", grad_mid_gathered, back_out, preferred_element_type=jnp.float32
    ).astype(jnp.bfloat16)
    grad_queries, grad_keys_all, grad_values_all = lax.map(
        attend_backward,
        (queries, keys_heads, values_heads, log_total, grad_mixed.reshape(head_shape)),
    )
    grad_keys_own, grad_values_own = (
        lax.psum_scatter(
            grad_keys_all.reshape(group_images, image_patches, local_width).astype(jnp.bfloat16),
            "context",
            scatter_dimension=1,
            tiled=True,
        ).astype(jnp.float32),
        lax.psum_scatter(
            grad_values_all.reshape(group_images, image_patches, local_width).astype(jnp.bfloat16),
            "context",
            scatter_dimension=1,
            tiled=True,
        ).astype(jnp.float32),
    )
    grad_queries_pre = rotate_back(grad_queries, cosine, sine).reshape(
        group_images, local_patches, local_width
    )
    grad_keys_pre = rotate_back(grad_keys_own.reshape(head_shape), cosine, sine).reshape(
        group_images, local_patches, local_width
    )
    gradient_of_projection_output = jnp.stack(
        [grad_queries_pre, grad_keys_pre, grad_values_own], axis=2
    ).astype(jnp.bfloat16)
    qkv_bias_own = jnp.sum(gradient_of_projection_output, axis=(0, 1), dtype=jnp.float32)
    qkv_weight_part = jnp.einsum(
        "brj,brto->jto",
        collected_first_normed,
        gradient_of_projection_output,
        preferred_element_type=jnp.float32,
    )
    shard_portion = gradient_of_projection_output
    grad_normed_one = lax.psum_scatter(
        jnp.einsum(
            "ufzc,lzc->ufl",
            shard_portion,
            backward_query_key_value,
            preferred_element_type=jnp.float32,
        ).astype(jnp.bfloat16),
        "tensor",
        scatter_dimension=0,
        tiled=True,
    ).astype(jnp.float32)
    grad_in_norm, gain_one_part, shift_one_part = norm_backward(
        grad_normed_one, unit_one, scale_one, attn_norm_gain
    )
    grad_input = grad_middle + grad_in_norm
    grad_qkv_weight, grad_fc1_weight = (
        lax.psum_scatter(qkv_weight_part, ("shard", "context"), scatter_dimension=0, tiled=True),
        lax.psum_scatter(fc1_weight_part, ("shard", "context"), scatter_dimension=0, tiled=True),
    )
    grad_out_weight, grad_fc2_weight = (
        lax.psum_scatter(out_weight_part, ("shard", "context"), scatter_dimension=1, tiled=True),
        lax.psum_scatter(fc2_weight_part, ("shard", "context"), scatter_dimension=1, tiled=True),
    )
    qkv_bias_slot = lax.dynamic_update_slice_in_dim(
        jnp.zeros_like(query_key_value_bias), qkv_bias_own, tensor_rank * local_width, 1
    )
    fc1_bias_slot = lax.dynamic_update_slice_in_dim(
        jnp.zeros_like(fc1_bias), fc1_bias_own, tensor_rank * local_units, 0
    )
    (
        grad_attn_norm_gain,
        grad_attn_norm_bias,
        grad_qkv_bias,
        grad_out_bias,
        grad_mlp_norm_gain,
        grad_mlp_norm_bias,
        grad_fc1_bias,
        grad_fc2_bias,
    ) = lax.psum(
        (
            gain_one_part,
            shift_one_part,
            qkv_bias_slot,
            out_bias_part,
            gain_two_part,
            shift_two_part,
            fc1_bias_slot,
            fc2_bias_part,
        ),
        ("shard", "tensor", "context"),
    )
    return (
        block_out,
        grad_input,
        grad_attn_norm_gain,
        grad_attn_norm_bias,
        grad_qkv_weight,
        grad_qkv_bias,
        grad_out_weight,
        grad_out_bias,
        grad_mlp_norm_gain,
        grad_mlp_norm_bias,
        grad_fc1_weight,
        grad_fc1_bias,
        grad_fc2_weight,
        grad_fc2_bias,
    )


def solution(mesh):
    placed = (
        P(("shard", "tensor"), "context", None),
        P("shard", "context"),
        P("shard", "context"),
        P(),
        P(),
        P(("shard", "context"), None, "tensor"),
        P(),
        P("tensor", ("shard", "context")),
        P(),
        P(),
        P(),
        P(("shard", "context"), "tensor"),
        P(),
        P("tensor", ("shard", "context")),
        P(),
        P(("shard", "tensor"), "context", None),
    )
    return jax.shard_map(
        on_device,
        mesh=mesh,
        in_specs=placed,
        out_specs=(
            P(("shard", "tensor"), "context", None),
            P(("shard", "tensor"), "context", None),
            P(),
            P(),
            P(("shard", "context"), None, "tensor"),
            P(),
            P("tensor", ("shard", "context")),
            P(),
            P(),
            P(),
            P(("shard", "context"), "tensor"),
            P(),
            P("tensor", ("shard", "context")),
            P(),
        ),
        check_vma=False,
    )
```

profile of v0, /device:TPU:10, one launch (start us, length us, event | category | flops | bytes accessed | tf_op | source)
XLA Modules:
  0.0 1782.6 jit_solution(12670248808709686272)
XLA Ops:
  13.8 12.1 all-gather.12.cloned.1.call-done
  25.9 85.0 %all-gather.14.cloned.1.call-done = bf16[1280,3,640]{2,0,1:T(8,128)(2,1)} async-done(((bf16[80,3,640]{2,0,1:T(8,128)(2,1)}), bf16[1280,3,640]{2,0,1:T(8,128)(2,1)}) %all-gather.14.cloned.1.call-update) | async-done | bytes 4915216 | tf_op jit(solution)/shard_map/all_gather | solution.py:112
  110.9 8.8 broadcast_add_fusion
  128.0 5.0 fusion.107
  146.3 4.2 fusion.95
  152.9 8.1 all-gather.30.cloned.1.call-done
  160.9 4.4 copy.74
  165.3 36.0 %all-gather.16.cloned.1.call-done = bf16[2,1024,640]{2,1,0:T(8,128)(2,1)} async-done(((bf16[2,512,640]{2,1,0:T(8,128)(2,1)}), bf16[2,1024,640]{2,1,0:T(8,128)(2,1)}) %all-gather.16.cloned.1.call-update) | async-done | bytes 2621456 | tf_op jit(solution)/shard_map/all_gather | solution.py:147
  204.3 24.4 %while.28 = (s32[]{:T(128)}, bf16[2,512,8,80]{1,3,2,0:T(8,128)(2,1)}, f32[2,8,512]{2,1,0:T(8,128)S(1)}, bf16[2,1024,8,80]{1,3,2,0:T(8,128)(2,1)}, bf16[2,512,8,8...) while((s32[]{:T(128)}, bf16[2,512,8,80]{1,3,2,0:T(8,128)(2,1)}, ...), condition=%wide.region_5.6_spmd.clone, body=%wide.region_2.5_spmd.sunk.clone | while | flops 1379921920 | bytes 65538156 | solution.py:154
  211.5 5.0 fusion.150
  223.7 5.0 fusion.150
  228.8 33.3 %all-gather.18.cloned.1.call-done = bf16[640,1280]{0,1:T(8,128)(2,1)} async-done(((bf16[640,80]{0,1:T(8,128)(2,1)}), bf16[640,1280]{0,1:T(8,128)(2,1)}) %all-gather.18.cloned.1.call-update) | async-done | bytes 1638416 | tf_op jit(solution)/shard_map/all_gather | solution.py:113
  262.1 5.7 convolution_convert_fusion
  268.6 9.9 reduce-scatter.11.cloned.1.call-done
  285.2 92.4 %all-gather.22.cloned.1.call-done = bf16[1280,2560]{1,0:T(8,128)(2,1)} async-done(((bf16[80,2560]{1,0:T(8,128)(2,1)}), bf16[1280,2560]{1,0:T(8,128)(2,1)}) %all-gather.22.cloned.1.call-update) | async-done | bytes 6553616 | tf_op jit(solution)/shard_map/all_gather | solution.py:114
  377.6 12.6 all-gather.20.cloned.1.call-done
  390.3 12.7 fusion.50
  404.4 99.0 %all-gather.24.cloned.1.call-done = bf16[2560,1280]{0,1:T(8,128)(2,1)} async-done(((bf16[2560,80]{0,1:T(8,128)(2,1)}), bf16[2560,1280]{0,1:T(8,128)(2,1)}) %all-gather.24.cloned.1.call-update) | async-done | bytes 6553616 | tf_op jit(solution)/shard_map/all_gather | solution.py:115
  503.4 14.2 convert_reduce_fusion
  519.9 11.1 fusion.58
  531.1 14.1 fusion.61
  549.9 5.2 reduce-scatter.13.cloned.1.call-done
  555.1 5.3 fusion.106
  563.2 12.6 all-gather.28.cloned.1.call-done
  575.8 5.5 fusion.99
  583.7 82.4 %while.29 = (s32[]{:T(128)}, f32[2,512,8,80]{1,3,2,0:T(8,128)}, bf16[2,1024,8,80]{1,3,2,0:T(8,128)(2,1)}, bf16[2,1024,8,80]{1,3,2,0:T(8,128)(2,1)}, bf16[2,1024,...) while((s32[]{:T(128)}, f32[2,512,8,80]{1,3,2,0:T(8,128)}, ...), condition=%wide.region_15.16_spmd.clone, body=%wide.region_13.15_spmd.sunk.clone | while | flops 3406753792 | bytes 225039664 | solution.py:229
  593.3 9.9 multiply_reduce_fusion.8
  603.2 8.1 multiply_convert_fusion.7
  617.3 6.1 fusion.160
  630.4 4.2 bitcast_dynamic-update-slice_fusion.11
  634.6 9.9 multiply_reduce_fusion.8
  644.5 8.1 multiply_convert_fusion.7
  658.5 6.1 fusion.160
  666.1 4.4 copy.82
  670.6 4.4 copy.86
  675.1 33.3 %reduce-scatter.17.cloned.1.call-done = bf16[2,512,640]{2,1,0:T(8,128)(2,1)} async-done(((bf16[2,1024,640]{2,1,0:T(8,128)(2,1)}), bf16[2,512,640]{2,1,0:T(8,128)(2,1)}) %reduce-scatter.17.cloned.1.call-update) | async-done | bytes 1310736 | tf_op jit(solution)/shard_map/reduce_scatter | solution.py:234
  730.3 18.5 %reduce-scatter.19.cloned.1.call-done = bf16[2,512,640]{2,1,0:T(8,128)(2,1)} async-done(((bf16[2,1024,640]{2,1,0:T(8,128)(2,1)}), bf16[2,512,640]{2,1,0:T(8,128)(2,1)}) %reduce-scatter.19.cloned.1.call-update) | async-done | bytes 1310736 | tf_op jit(solution)/shard_map/reduce_scatter | solution.py:240
  748.8 9.9 bitcast_convert_fusion
  760.0 5.7 convolution_bitcast_fusion.3
  773.9 13.8 convolution_bitcast_fusion
  787.7 12.8 convolution_bitcast_fusion.1
  800.6 10.3 convolution_bitcast_fusion.2
  812.3 4.2 fusion.80
  816.5 35.3 %reduce-scatter.25.cloned.1.call-done = f32[640,80]{0,1:T(8,128)} async-done(((f32[640,1280]{0,1:T(8,128)}), f32[640,80]{0,1:T(8,128)}) %reduce-scatter.25.cloned.1.call-update) | async-done | bytes 204816 | tf_op jit(solution)/shard_map/reduce_scatter | solution.py:284
  851.8 140.3 %all-reduce.3.cloned.1.call-done = (f32[1280]{0:T(1024)}, f32[1280]{0:T(1024)}, f32[3,1280]{1,0:T(4,128)}, f32[1280]{0:T(1024)}, f32[1280]{0:T(1024)}, /*index=5*/f32[1280]{0:T(1024)}, f32[5120]{0:T(1024)}, f32[1280]{0:T(1024)}) async-done(((f32[1280]{0:T(1024)}, f32[1280]{0:T(1024)}, f32[3,1280]{1,0:T(4,128)}, f32[1280]{0:T(1024)}, f32[1280]{0:T(1024)}, /*index=5*/f32[1280]{0:T(1024)}, f32[5120]{0:T(1024)}, ...) | async-done | bytes 66576 | tf_op jit(solution)/shard_map/psum | solution.py:302
  992.1 279.6 %reduce-scatter.29.cloned.1.call-done = f32[2560,80]{0,1:T(8,128)} async-done(((f32[2560,1280]{0,1:T(8,128)}), f32[2560,80]{0,1:T(8,128)}) %reduce-scatter.29.cloned.1.call-update) | async-done | bytes 819216 | tf_op jit(solution)/shard_map/reduce_scatter | solution.py:285
  1271.7 280.3 %reduce-scatter.27.cloned.1.call-done = f32[80,2560]{1,0:T(8,128)} async-done(((f32[1280,2560]{1,0:T(8,128)}), f32[80,2560]{1,0:T(8,128)}) %reduce-scatter.27.cloned.1.call-update) | async-done | bytes 819216 | tf_op jit(solution)/shard_map/reduce_scatter | solution.py:281
  1552.0 213.1 %reduce-scatter.23.cloned.1.call-done = f32[80,3,640]{2,0,1:T(8,128)} async-done(((f32[1280,3,640]{2,0,1:T(8,128)}), f32[80,3,640]{2,0,1:T(8,128)}) %reduce-scatter.23.cloned.1.call-update) | async-done | bytes 614416 | tf_op jit(solution)/shard_map/reduce_scatter | solution.py:280
  (229 shorter events, 141.7 us)
Async XLA Ops:
  7.2 6.6 copy-start
  7.2 4.2 copy-start.5
  7.2 4.1 copy-start.31
  7.2 4.1 copy-start.40
  7.2 18.7 %all-gather.12.cloned.1.call-start = ((), (), s32[]{:S(2)}) async-start(), calls=%async_computation.10 | async-start | bytes 3932160 | tf_op jit(solution)/shard_map/all_gather | solution.py:119
  13.0 97.9 %all-gather.14.cloned.1.call-start = ((), (), s32[]{:S(2)}) async-start(), calls=%async_computation.11 | async-start | bytes 5222400 | tf_op jit(solution)/shard_map/all_gather | solution.py:112
  13.7 147.2 %all-gather.30.cloned.1.call-start = ((), (), s32[]{:S(2)}) async-start(), calls=%async_computation.29 | async-start | bytes 3932160 | tf_op jit(solution)/shard_map/all_gather | solution.py:148
  124.0 77.4 %all-gather.16.cloned.1.call-start = ((), (), s32[]{:S(2)}) async-start(), calls=%async_computation.12 | async-start | bytes 3932160 | tf_op jit(solution)/shard_map/all_gather | solution.py:147
  125.4 14.4 copy-start.21
  125.4 14.4 copy-start.24
  150.5 111.6 %all-gather.18.cloned.1.call-start = ((), (), s32[]{:S(2)}) async-start(), calls=%async_computation.13 | async-start | bytes 1740800 | tf_op jit(solution)/shard_map/all_gather | solution.py:113
  151.1 127.4 %reduce-scatter.11.cloned.1.call-start = ((), (), s32[]{:S(2)}) async-start(), calls=%async_computation.14 | async-start | bytes 3932160 | tf_op jit(solution)/shard_map/reduce_scatter | solution.py:157
  207.9 3.6 copy-start.11
  220.1 3.6 copy-start.11
  267.8 10.7 copy-start.27
  267.8 109.8 %all-gather.22.cloned.1.call-start = ((), (), s32[]{:S(2)}) async-start(), calls=%async_computation.16 | async-start | bytes 6963200 | tf_op jit(solution)/shard_map/all_gather | solution.py:114
  267.9 13.8 copy-start.41
  268.6 13.1 copy-start.30
  268.6 121.7 %all-gather.20.cloned.1.call-start = ((), (), s32[]{:S(2)}) async-start(), calls=%async_computation.15 | async-start | bytes 3932160 | tf_op jit(solution)/shard_map/all_gather | solution.py:167
  283.6 120.8 %all-gather.26.cloned.1.call-start = ((), (), s32[]{:S(2)}) async-start(), calls=%async_computation.19 | async-start | bytes 3932160 | tf_op jit(solution)/shard_map/all_gather | solution.py:193
  284.3 219.1 %all-gather.24.cloned.1.call-start = ((), (), s32[]{:S(2)}) async-start(), calls=%async_computation.17 | async-start | bytes 6963200 | tf_op jit(solution)/shard_map/all_gather | solution.py:115
  284.9 260.8 %reduce-scatter.15.cloned.1.call-start = ((), (), s32[]{:S(2)}) async-start(), calls=%async_computation.20 | async-start | bytes 3932160 | tf_op jit(solution)/shard_map/reduce_scatter | solution.py:207
  285.2 245.9 %copy-start.37 = (f32[2560]{0:T(1024)}, f32[2560]{0:T(1024)S(1)}, u32[]{:S(2)}) copy-start(f32[2560]{0:T(1024)S(1)} %dynamic_slice.34) | copy-start | bytes 30724
  531.0 24.0 %reduce-scatter.13.cloned.1.call-start = ((), (), s32[]{:S(2)}) async-start(), calls=%async_computation.18 | async-start | bytes 3932160 | tf_op jit(solution)/shard_map/reduce_scatter | solution.py:176
  545.2 9.9 copy-start.42
  545.2 30.6 %all-gather.28.cloned.1.call-start = ((), (), s32[]{:S(2)}) async-start(), calls=%async_computation.21 | async-start | bytes 3932160 | tf_op jit(solution)/shard_map/all_gather | solution.py:220
  563.1 145.3 %reduce-scatter.17.cloned.1.call-start = ((), (), s32[]{:S(2)}) async-start(), calls=%async_computation.22 | async-start | bytes 3932160 | tf_op jit(solution)/shard_map/reduce_scatter | solution.py:234
  585.1 4.0 copy-start.9
  603.2 11.4 copy-start.8
  626.4 4.0 copy-start.9
  644.5 11.4 copy-start.8
  670.6 78.2 %reduce-scatter.19.cloned.1.call-start = ((), (), s32[]{:S(2)}) async-start(), calls=%async_computation.23 | async-start | bytes 3932160 | tf_op jit(solution)/shard_map/reduce_scatter | solution.py:240
  675.0 36.4 %copy-start.18 = (f32[2,512,8,80]{1,3,2,0:T(8,128)S(1)}, f32[2,512,8,80]{1,3,2,0:T(8,128)}, u32[]{:S(2)}) copy-start(f32[2,512,8,80]{1,3,2,0:T(8,128)} %get-tuple-element.98) | copy-start | bytes 7864324
  675.0 36.4 %copy-start.25 = (f32[2,512,80]{1,2,0:T(8,128)S(1)}, f32[2,512,80]{1,2,0:T(8,128)}, u32[]{:S(2)}) copy-start(f32[2,512,80]{1,2,0:T(8,128)} %copy-done.24) | copy-start | bytes 983044
  675.0 95.6 %reduce-scatter.21.cloned.1.call-start = ((), (), s32[]{:S(2)}) async-start(), calls=%async_computation.24 | async-start | bytes 3932160 | tf_op jit(solution)/shard_map/reduce_scatter | solution.py:264
  758.7 93.1 %reduce-scatter.25.cloned.1.call-start = ((), (), s32[]{:S(2)}) async-start(), calls=%async_computation.26 | async-start | bytes 3481600 | tf_op jit(solution)/shard_map/reduce_scatter | solution.py:284
  765.8 4.8 copy-start.7
  765.8 4.8 copy-start.32
  765.8 4.8 copy-start.34
  765.8 4.8 copy-start.36
  765.8 226.3 %all-reduce.3.cloned.1.call-start = ((), (), s32[]{:S(2)}) async-start(), calls=%async_computation.30 | async-start | bytes 180224 | tf_op jit(solution)/shard_map/psum | solution.py:302
  767.3 6.5 copy-start.29
  767.3 6.6 copy-start.38
  769.4 4.4 copy-start.28
  773.8 497.9 %reduce-scatter.29.cloned.1.call-start = ((), (), s32[]{:S(2)}) async-start(), calls=%async_computation.28 | async-start | bytes 13926400 | tf_op jit(solution)/shard_map/reduce_scatter | solution.py:285
  787.7 764.3 %reduce-scatter.27.cloned.1.call-start = ((), (), s32[]{:S(2)}) async-start(), calls=%async_computation.27 | async-start | bytes 13926400 | tf_op jit(solution)/shard_map/reduce_scatter | solution.py:281
  800.6 964.5 %reduce-scatter.23.cloned.1.call-start = ((), (), s32[]{:S(2)}) async-start(), calls=%async_computation.25 | async-start | bytes 10444800 | tf_op jit(solution)/shard_map/reduce_scatter | solution.py:280
  811.0 964.5 %copy-start.1 = (f32[3,1280]{1,0:T(4,128)S(1)}, f32[3,1280]{1,0:T(4,128)}, u32[]{:S(2)}) copy-start(f32[3,1280]{1,0:T(4,128)} %param.26) | copy-start | bytes 46084
  (28 other events, 58.6 us)
Sparse Core Ops, SparseCore 0:
  13.1 12.7 all-gather.11
  28.6 82.2 all-gather.13
  124.1 36.7 all-gather.29
  162.3 38.9 all-gather.15
  203.9 58.1 all-gather.17
  267.9 10.5 reduce-scatter.10
  281.2 96.4 all-gather.21
  379.8 10.4 all-gather.19
  391.8 12.5 all-gather.25
  406.9 96.4 all-gather.23
  531.1 9.7 reduce-scatter.14
  545.3 9.7 reduce-scatter.12
  563.2 12.5 all-gather.27
  670.7 37.6 reduce-scatter.16
  711.0 37.6 reduce-scatter.18
  758.8 11.7 reduce-scatter.20
  773.3 78.4 reduce-scatter.24
  859.2 132.8 all-reduce.2
  995.0 276.6 reduce-scatter.28
  1274.4 277.5 reduce-scatter.26
  1554.9 210.1 reduce-scatter.22
where the time goes:
time: 1790 us; the launch traced here: 1780 us
  waiting for transfers between devices  1410 us (79%)
  matrix products  195 us (11%)
  local copies, waits for them, and re-layouts  79.3 us (4%)
  other arithmetic  78.1 us (4%)
    reduce_scatter x1, waiting for transfers between devices, on_device(): lax.psum_scatter(fc1_weight_part, ('shard', 'context'), scatter_dimension...  280 us
    reduce_scatter x1, waiting for transfers between devices, on_device(): lax.psum_scatter(fc2_weight_part, ('shard', 'context'), scatter_dimension...  280 us
    reduce_scatter x1, waiting for transfers between devices, on_device(): lax.psum_scatter(qkv_weight_part, ('shard', 'context'), scatter_dimension...  213 us
    psum x1, waiting for transfers between devices, on_device(): lax.psum((gain_one_part, shift_one_part, qkv_bias_slot, out_bias_part, ga...  140 us
    all_gather x1, waiting for transfers between devices, on_device(): lax.all_gather(fc2_weight, ('shard', 'context'), axis=1, tiled=True)  99 us
    all_gather x1, waiting for transfers between devices, on_device(): lax.all_gather(fc1_weight, ('shard', 'context'), axis=0, tiled=True)  92.4 us
    all_gather x1, waiting for transfers between devices, on_device(): lax.all_gather(query_key_value_weight, ('shard', 'context'), axis=0, tile...  85 us
    all_gather x1, waiting for transfers between devices, on_device(): lax.all_gather(keys_flat, 'context', axis=1, tiled=True)  36 us
  transfers between devices with their start and end apart: 21, of which 20 were waited for; matrix products, arithmetic and copies ran while one was open for 10% of the time, Pallas kernels for 0%

commit v1 on v0

--- a/solution.py
+++ b/solution.py
@@ -4,6 +4,22 @@
 from jax.sharding import PartitionSpec as P
 
 HEAD_DIM = 80
+
+
+def collect(x, axis, dim):
+    ways, here, step = (lax.axis_size(axis), lax.axis_index(axis), x.shape[dim])
+    lengths = [n * ways if d == dim else n for d, n in enumerate(x.shape)]
+    full = lax.dynamic_update_slice_in_dim(jnp.zeros(lengths, x.dtype), x, here * step, axis=dim)
+    going_up = going_down = x
+    for far in range(1, ways // 2 + 1):
+        going_up = lax.ppermute(going_up, axis, [(d, (d + 1) % ways) for d in range(ways)])
+        full = lax.dynamic_update_slice_in_dim(full, going_up, (here - far) % ways * step, axis=dim)
+        if 2 * far < ways:
+            going_down = lax.ppermute(going_down, axis, [(d, (d - 1) % ways) for d in range(ways)])
+            full = lax.dynamic_update_slice_in_dim(
+                full, going_down, (here + far) % ways * step, axis=dim
+            )
+    return full
 
 
 def normalize(field, gain, shift):
@@ -109,7 +125,7 @@
     head_count = local_width // HEAD_DIM
     tensor_rank = lax.axis_index("tensor")
     complete_query_key_value, full_out, full_fc1, full_fc2 = (
-        lax.all_gather(query_key_value_weight, ("shard", "context"), axis=0, tiled=True),
+        collect(query_key_value_weight, ("shard", "context"), 0),
         lax.all_gather(out_weight, ("shard", "context"), axis=1, tiled=True),
         lax.all_gather(fc1_weight, ("shard", "context"), axis=0, tiled=True),
         lax.all_gather(fc2_weight, ("shard", "context"), axis=1, tiled=True),

time: 1790 us -> 1900 us (1.061)
  waiting for transfers between devices: 1410 us -> 1500 us
    ppermute x0 -> x15, waiting for transfers between devices: none -> 75.1 us  [the longest x8 74.7 us: collect(): lax.ppermute(going_up, axis, [(d, (d + 1) % ways) for d in range(ways)])]
    all_gather x1, waiting for transfers between devices: 8.05 us -> 36.7 us  [on_device(): lax.all_gather(values_local, 'context', axis=1, tiled=True)]
    all_gather x1, waiting for transfers between devices: 85 us -> 62.7 us  [on_device(): lax.all_gather(query_key_value_weight, ('shard', 'context'), axis=0, tile...]
    reduce_scatter x1, waiting for transfers between devices: 18.5 us -> 38.1 us  [on_device(): lax.psum_scatter(grad_values_all.reshape(group_images, image_patches, loc...]
  transfers between devices with their start and end apart: 21 -> 36, of which waited for: 20 -> 28; matrix products, arithmetic and copies ran while one was open for 10% -> 9% of each run, Pallas kernels for 0% -> 0%
where the time goes in v1:
time: 1900 us; the launch traced here: 1890 us
  waiting for transfers between devices  1500 us (79%)
  matrix products  196 us (10%)
  local copies, waits for them, and re-layouts  88.8 us (5%)
  other arithmetic  78.4 us (4%)
    reduce_scatter x1, waiting for transfers between devices, on_device(): lax.psum_scatter(fc2_weight_part, ('shard', 'context'), scatter_dimension...  280 us
    reduce_scatter x1, waiting for transfers between devices, on_device(): lax.psum_scatter(fc1_weight_part, ('shard', 'context'), scatter_dimension...  280 us
    reduce_scatter x1, waiting for transfers between devices, on_device(): lax.psum_scatter(qkv_weight_part, ('shard', 'context'), scatter_dimension...  213 us
    psum x1, waiting for transfers between devices, on_device(): lax.psum((gain_one_part, shift_one_part, qkv_bias_slot, out_bias_part, ga...  140 us
    all_gather x1, waiting for transfers between devices, on_device(): lax.all_gather(fc2_weight, ('shard', 'context'), axis=1, tiled=True)  99.2 us
    all_gather x1, waiting for transfers between devices, on_device(): lax.all_gather(fc1_weight, ('shard', 'context'), axis=0, tiled=True)  92.7 us
    ppermute x8, waiting for transfers between devices, collect(): lax.ppermute(going_up, axis, [(d, (d + 1) % ways) for d in range(ways)])  74.7 us
    all_gather x1, waiting for transfers between devices, on_device(): lax.all_gather(query_key_value_weight, ('shard', 'context'), axis=0, tile...  62.7 us
  transfers between devices with their start and end apart: 36, of which 28 were waited for; matrix products, arithmetic and copies ran while one was open for 9% of the time, Pallas kernels for 0%

profile of v1, /device:TPU:10, one launch (start us, length us, event | category | flops | bytes accessed | tf_op | source)
XLA Modules:
  0.0 1892.3 jit_solution(13902857124684935445)
XLA Ops:
  12.8 10.3 collective-permute-done
  27.0 11.1 collective-permute-done.2
  47.6 5.4 collective-permute-done.4
  57.5 11.7 collective-permute-done.6
  76.3 9.1 collective-permute-done.8
  89.7 11.2 collective-permute-done.10
  105.2 11.3 collective-permute-done.12
  119.1 4.6 collective-permute-done.14
  124.5 8.8 broadcast_add_fusion
  154.8 4.7 fusion.95
  163.8 32.1 %all-gather.14.cloned.1.call-done = bf16[2,1024,640]{2,1,0:T(8,128)(2,1)} async-done(((bf16[2,512,640]{2,1,0:T(8,128)(2,1)}), bf16[2,1024,640]{2,1,0:T(8,128)(2,1)}) %all-gather.14.cloned.1.call-update) | async-done | bytes 2621456 | tf_op jit(solution)/shard_map/all_gather | solution.py:163
  195.9 4.5 copy.79
  200.4 36.7 %all-gather.30.cloned.1.call-done = bf16[2,1024,1,640]{3,1,2,0:T(8,128)(2,1)} async-done(((bf16[2,512,1,640]{3,1,2,0:T(8,128)(2,1)}), bf16[2,1024,1,640]{3,1,2,0:T(8,128)(2,1)}) %all-gather.30.cloned.1.call-update) | async-done | bytes 2621456 | tf_op jit(solution)/shard_map/all_gather | solution.py:164
  241.4 23.6 %while.28 = (s32[]{:T(128)}, bf16[2,512,8,80]{1,3,2,0:T(8,128)(2,1)S(1)}, f32[2,8,512]{2,1,0:T(8,128)S(1)}, bf16[2,1024,8,80]{1,3,2,0:T(8,128)(2,1)}, bf16[2,512...) while((s32[]{:T(128)}, bf16[2,512,8,80]{1,3,2,0:T(8,128)(2,1)S(1)}, ...), condition=%wide.region_5.6_spmd.clone, body=%wide.region_2.5_spmd.sunk.clone | while | flops 1379921920 | bytes 65538148 | solution.py:170
  265.0 32.8 %all-gather.16.cloned.1.call-done = bf16[640,1280]{0,1:T(8,128)(2,1)} async-done(((bf16[640,80]{0,1:T(8,128)(2,1)}), bf16[640,1280]{0,1:T(8,128)(2,1)}) %all-gather.16.cloned.1.call-update) | async-done | bytes 1638416 | tf_op jit(solution)/shard_map/all_gather | solution.py:129
  297.8 5.1 convolution_convert_fusion
  303.7 10.0 reduce-scatter.11.cloned.1.call-done
  320.0 92.7 %all-gather.20.cloned.1.call-done = bf16[1280,2560]{1,0:T(8,128)(2,1)} async-done(((bf16[80,2560]{1,0:T(8,128)(2,1)}), bf16[1280,2560]{1,0:T(8,128)(2,1)}) %all-gather.20.cloned.1.call-update) | async-done | bytes 6553616 | tf_op jit(solution)/shard_map/all_gather | solution.py:130
  412.7 12.6 all-gather.18.cloned.1.call-done
  425.4 12.7 fusion.50
  439.5 99.2 %all-gather.22.cloned.1.call-done = bf16[2560,1280]{0,1:T(8,128)(2,1)} async-done(((bf16[2560,80]{0,1:T(8,128)(2,1)}), bf16[2560,1280]{0,1:T(8,128)(2,1)}) %all-gather.22.cloned.1.call-update) | async-done | bytes 6553616 | tf_op jit(solution)/shard_map/all_gather | solution.py:131
  538.6 14.2 convert_reduce_fusion
  555.2 11.1 fusion.58
  566.3 14.1 fusion.61
  584.4 5.9 reduce-scatter.13.cloned.1.call-done
  590.3 5.1 fusion.106
  598.2 12.6 all-gather.26.cloned.1.call-done
  610.8 4.4 fusion.99
  616.7 76.5 %while.29 = (s32[]{:T(128)}, f32[2,512,8,80]{1,3,2,0:T(8,128)}, bf16[2,1024,8,80]{1,3,2,0:T(8,128)(2,1)}, bf16[2,1024,8,80]{1,3,2,0:T(8,128)(2,1)}, bf16[2,1024,...) while((s32[]{:T(128)}, f32[2,512,8,80]{1,3,2,0:T(8,128)}, ...), condition=%wide.region_15.16_spmd.clone, body=%wide.region_13.15_spmd.sunk.clone | while | flops 3406753792 | bytes 204068080 | solution.py:245
  620.6 9.9 multiply_reduce_fusion.8
  630.6 8.4 multiply_convert_fusion.7
  642.3 8.5 fusion.160
  658.9 9.9 multiply_reduce_fusion.8
  668.8 8.4 multiply_convert_fusion.7
  680.5 8.5 fusion.160
  702.0 33.5 %reduce-scatter.17.cloned.1.call-done = bf16[2,512,640]{2,1,0:T(8,128)(2,1)} async-done(((bf16[2,1024,640]{2,1,0:T(8,128)(2,1)}), bf16[2,512,640]{2,1,0:T(8,128)(2,1)}) %reduce-scatter.17.cloned.1.call-update) | async-done | bytes 1310736 | tf_op jit(solution)/shard_map/reduce_scatter | solution.py:250
  757.6 62.7 %all-gather.28.cloned.1.call-done = bf16[1280,3,640]{2,0,1:T(8,128)(2,1)} async-done(((bf16[80,3,640]{2,0,1:T(8,128)(2,1)}), bf16[1280,3,640]{2,0,1:T(8,128)(2,1)}) %all-gather.28.cloned.1.call-update) | async-done | bytes 4915216 | tf_op jit(solution)/shard_map/all_gather | solution.py:202
  820.3 38.1 %reduce-scatter.19.cloned.1.call-done = bf16[2,512,640]{2,1,0:T(8,128)(2,1)} async-done(((bf16[2,1024,640]{2,1,0:T(8,128)(2,1)}), bf16[2,512,640]{2,1,0:T(8,128)(2,1)}) %reduce-scatter.19.cloned.1.call-update) | async-done | bytes 1310736 | tf_op jit(solution)/shard_map/reduce_scatter | solution.py:256
  858.5 9.9 bitcast_convert_fusion
  869.7 5.7 convolution_bitcast_fusion.3
  883.6 13.1 convolution_bitcast_fusion.1
  897.5 13.6 convolution_bitcast_fusion
  911.1 10.2 convolution_bitcast_fusion.2
  926.9 35.5 %reduce-scatter.25.cloned.1.call-done = f32[640,80]{0,1:T(8,128)} async-done(((f32[640,1280]{0,1:T(8,128)}), f32[640,80]{0,1:T(8,128)}) %reduce-scatter.25.cloned.1.call-update) | async-done | bytes 204816 | tf_op jit(solution)/shard_map/reduce_scatter | solution.py:300
  962.4 139.5 %all-reduce.3.cloned.1.call-done = (f32[1280]{0:T(1024)}, f32[1280]{0:T(1024)}, f32[3,1280]{1,0:T(4,128)}, f32[1280]{0:T(1024)}, f32[1280]{0:T(1024)}, /*index=5*/f32[1280]{0:T(1024)}, f32[5120]{0:T(1024)}, f32[1280]{0:T(1024)}) async-done(((f32[1280]{0:T(1024)}, f32[1280]{0:T(1024)}, f32[3,1280]{1,0:T(4,128)}, f32[1280]{0:T(1024)}, f32[1280]{0:T(1024)}, /*index=5*/f32[1280]{0:T(1024)}, f32[5120]{0:T(1024)}, ...) | async-done | bytes 66576 | tf_op jit(solution)/shard_map/psum | solution.py:318
  1101.9 279.6 %reduce-scatter.27.cloned.1.call-done = f32[80,2560]{1,0:T(8,128)} async-done(((f32[1280,2560]{1,0:T(8,128)}), f32[80,2560]{1,0:T(8,128)}) %reduce-scatter.27.cloned.1.call-update) | async-done | bytes 819216 | tf_op jit(solution)/shard_map/reduce_scatter | solution.py:297
  1381.5 280.3 %reduce-scatter.29.cloned.1.call-done = f32[2560,80]{0,1:T(8,128)} async-done(((f32[2560,1280]{0,1:T(8,128)}), f32[2560,80]{0,1:T(8,128)}) %reduce-scatter.29.cloned.1.call-update) | async-done | bytes 819216 | tf_op jit(solution)/shard_map/reduce_scatter | solution.py:301
  1661.8 213.1 %reduce-scatter.23.cloned.1.call-done = f32[80,3,640]{2,0,1:T(8,128)} async-done(((f32[1280,3,640]{2,0,1:T(8,128)}), f32[80,3,640]{2,0,1:T(8,128)}) %reduce-scatter.23.cloned.1.call-update) | async-done | bytes 614416 | tf_op jit(solution)/shard_map/reduce_scatter | solution.py:296
  (276 shorter events, 194.3 us)
Async XLA Ops:
  7.2 45.8 %copy-start = (f32[3,1280]{1,0:T(4,128)S(1)}, f32[3,1280]{1,0:T(4,128)}, u32[]{:S(2)}) copy-start(f32[3,1280]{1,0:T(4,128)} %param.26) | copy-start | bytes 46084
  7.2 16.0 copy-start.3
  7.2 16.0 copy-start.33
  7.2 16.0 copy-start.42
  7.2 117.2 %all-gather.12.cloned.1.call-start = ((), (), s32[]{:S(2)}) async-start(), calls=%async_computation.10 | async-start | bytes 3932160 | tf_op jit(solution)/shard_map/all_gather | solution.py:135
  7.3 15.9 collective-permute-start
  8.8 16.5 collective-permute-start.1
  23.1 16.5 copy-start.27
  23.1 14.9 collective-permute-start.2
  24.8 171.1 %all-gather.14.cloned.1.call-start = ((), (), s32[]{:S(2)}) async-start(), calls=%async_computation.11 | async-start | bytes 3932160 | tf_op jit(solution)/shard_map/all_gather | solution.py:163
  25.3 16.8 collective-permute-start.3
  38.1 14.9 collective-permute-start.4
  39.7 107.4 %copy-start.16 = (f32[2,512,80]{1,2,0:T(8,128)}, f32[2,512,80]{1,2,0:T(8,128)S(1)}, u32[]{:S(2)}) copy-start(f32[2,512,80]{1,2,0:T(8,128)S(1)} %get-tuple-element.184) | copy-start | bytes 983044
  39.7 107.4 %copy-start.19 = (f32[2,512,80]{1,2,0:T(8,128)}, f32[2,512,80]{1,2,0:T(8,128)S(1)}, u32[]{:S(2)}) copy-start(f32[2,512,80]{1,2,0:T(8,128)S(1)} %get-tuple-element.185) | copy-start | bytes 983044
  42.1 11.6 collective-permute-start.5
  52.9 16.2 collective-permute-start.6
  53.7 18.8 collective-permute-start.7
  69.1 16.3 collective-permute-start.8
  72.6 14.4 collective-permute-start.9
  85.4 15.5 collective-permute-start.10
  87.0 15.5 collective-permute-start.11
  100.9 15.7 collective-permute-start.12
  102.4 15.9 collective-permute-start.13
  116.6 7.1 collective-permute-start.14
  159.5 77.6 %all-gather.30.cloned.1.call-start = ((), (), s32[]{:S(2)}) async-start(), calls=%async_computation.29 | async-start | bytes 3932160 | tf_op jit(solution)/shard_map/all_gather | solution.py:164
  162.5 135.3 %all-gather.16.cloned.1.call-start = ((), (), s32[]{:S(2)}) async-start(), calls=%async_computation.12 | async-start | bytes 1740800 | tf_op jit(solution)/shard_map/all_gather | solution.py:129
  163.1 150.6 %reduce-scatter.11.cloned.1.call-start = ((), (), s32[]{:S(2)}) async-start(), calls=%async_computation.13 | async-start | bytes 3932160 | tf_op jit(solution)/shard_map/reduce_scatter | solution.py:173
  265.0 32.8 %copy-start.6 = (bf16[2,512,8,80]{1,3,2,0:T(8,128)(2,1)}, bf16[2,512,8,80]{1,3,2,0:T(8,128)(2,1)S(1)}, u32[]{:S(2)}) copy-start(bf16[2,512,8,80]{1,3,2,0:T(8,128)(2,1)S(1)} %get-tuple-element.425) | copy-start | bytes 3932164
  265.0 38.0 %copy-start.24 = (bf16[2,512,8,80]{1,3,2,0:T(8,128)(2,1)}, bf16[2,512,8,80]{1,3,2,0:T(8,128)(2,1)S(1)}, u32[]{:S(2)}) copy-start(bf16[2,512,8,80]{1,3,2,0:T(8,128)(2,1)S(1)} %get-tuple-element.96) | copy-start | bytes 3932164
  303.0 109.7 %all-gather.20.cloned.1.call-start = ((), (), s32[]{:S(2)}) async-start(), calls=%async_computation.15 | async-start | bytes 6963200 | tf_op jit(solution)/shard_map/all_gather | solution.py:130
  303.6 121.7 %all-gather.18.cloned.1.call-start = ((), (), s32[]{:S(2)}) async-start(), calls=%async_computation.14 | async-start | bytes 3932160 | tf_op jit(solution)/shard_map/all_gather | solution.py:183
  318.2 121.2 %all-gather.24.cloned.1.call-start = ((), (), s32[]{:S(2)}) async-start(), calls=%async_computation.18 | async-start | bytes 3932160 | tf_op jit(solution)/shard_map/all_gather | solution.py:209
  319.0 219.6 %all-gather.22.cloned.1.call-start = ((), (), s32[]{:S(2)}) async-start(), calls=%async_computation.16 | async-start | bytes 6963200 | tf_op jit(solution)/shard_map/all_gather | solution.py:131
  319.7 261.2 %reduce-scatter.15.cloned.1.call-start = ((), (), s32[]{:S(2)}) async-start(), calls=%async_computation.19 | async-start | bytes 3932160 | tf_op jit(solution)/shard_map/reduce_scatter | solution.py:223
  320.0 246.3 %copy-start.39 = (f32[2560]{0:T(1024)}, f32[2560]{0:T(1024)S(1)}, u32[]{:S(2)}) copy-start(f32[2560]{0:T(1024)S(1)} %dynamic_slice.34) | copy-start | bytes 30724
  566.3 24.0 %reduce-scatter.13.cloned.1.call-start = ((), (), s32[]{:S(2)}) async-start(), calls=%async_computation.17 | async-start | bytes 3932160 | tf_op jit(solution)/shard_map/reduce_scatter | solution.py:192
  580.4 30.4 %all-gather.26.cloned.1.call-start = ((), (), s32[]{:S(2)}) async-start(), calls=%async_computation.20 | async-start | bytes 3932160 | tf_op jit(solution)/shard_map/all_gather | solution.py:236
  598.2 137.3 %reduce-scatter.17.cloned.1.call-start = ((), (), s32[]{:S(2)}) async-start(), calls=%async_computation.21 | async-start | bytes 3932160 | tf_op jit(solution)/shard_map/reduce_scatter | solution.py:250
  697.6 122.7 %all-gather.28.cloned.1.call-start = ((), (), s32[]{:S(2)}) async-start(), calls=%async_computation.23 | async-start | bytes 5222400 | tf_op jit(solution)/shard_map/all_gather | solution.py:202
  698.2 160.3 %reduce-scatter.19.cloned.1.call-start = ((), (), s32[]{:S(2)}) async-start(), calls=%async_computation.22 | async-start | bytes 3932160 | tf_op jit(solution)/shard_map/reduce_scatter | solution.py:256
  701.9 36.5 %copy-start.20 = (f32[2,512,80]{1,2,0:T(8,128)S(1)}, f32[2,512,80]{1,2,0:T(8,128)}, u32[]{:S(2)}) copy-start(f32[2,512,80]{1,2,0:T(8,128)} %copy-done.19) | copy-start | bytes 983044
  701.9 178.4 %reduce-scatter.21.cloned.1.call-start = ((), (), s32[]{:S(2)}) async-start(), calls=%async_computation.24 | async-start | bytes 3932160 | tf_op jit(solution)/shard_map/reduce_scatter | solution.py:280
  868.4 94.0 %reduce-scatter.25.cloned.1.call-start = ((), (), s32[]{:S(2)}) async-start(), calls=%async_computation.26 | async-start | bytes 3481600 | tf_op jit(solution)/shard_map/reduce_scatter | solution.py:300
  875.5 226.4 %all-reduce.3.cloned.1.call-start = ((), (), s32[]{:S(2)}) async-start(), calls=%async_computation.30 | async-start | bytes 180224 | tf_op jit(solution)/shard_map/psum | solution.py:318
  883.6 497.9 %reduce-scatter.27.cloned.1.call-start = ((), (), s32[]{:S(2)}) async-start(), calls=%async_computation.27 | async-start | bytes 13926400 | tf_op jit(solution)/shard_map/reduce_scatter | solution.py:297
  896.8 765.0 %reduce-scatter.29.cloned.1.call-start = ((), (), s32[]{:S(2)}) async-start(), calls=%async_computation.28 | async-start | bytes 13926400 | tf_op jit(solution)/shard_map/reduce_scatter | solution.py:301
  911.1 963.7 %reduce-scatter.23.cloned.1.call-start = ((), (), s32[]{:S(2)}) async-start(), calls=%async_computation.25 | async-start | bytes 10444800 | tf_op jit(solution)/shard_map/reduce_scatter | solution.py:296
  921.4 963.8 %copy-start.1 = (f32[3,1280]{1,0:T(4,128)S(1)}, f32[3,1280]{1,0:T(4,128)}, u32[]{:S(2)}) copy-start(f32[3,1280]{1,0:T(4,128)} %param.26) | copy-start | bytes 46084
  (43 other events, 264.9 us)
Sparse Core Ops, SparseCore 0:
  24.9 12.3 all-gather.11
  159.6 36.2 all-gather.13
  198.0 38.9 all-gather.29
  239.6 58.1 all-gather.15
  303.1 10.5 reduce-scatter.10
  316.2 96.4 all-gather.19
  414.8 10.4 all-gather.17
  426.9 12.5 all-gather.23
  442.1 96.4 all-gather.21
  566.4 9.7 reduce-scatter.14
  580.5 9.7 reduce-scatter.12
  598.3 12.4 all-gather.25
  697.7 37.6 reduce-scatter.16
  738.0 82.2 all-gather.27
  823.0 35.4 reduce-scatter.18
  868.5 11.7 reduce-scatter.20
  883.1 79.2 reduce-scatter.24
  969.8 132.0 all-reduce.2
  1104.8 276.6 reduce-scatter.26
  1384.2 277.5 reduce-scatter.28
  1664.7 210.1 reduce-scatter.22
